TPU v7x, 512 devices: a whole 4x4x16 slice. The times are simulated.
512 devices in a mesh: tau: 8 (over z_lo), row: 8 (over y, core), col: 8 (over x, z_hi).
Axes of the slice: x: 4, y: 4, z: 16 (z_hi: 2, z_lo: 8; z = z_hi * 8 + z_lo), core: 2. Of those that a mesh axis runs over, the one named last changes fastest.
Arguments:
- occupied: bfloat16 [8, 1024, 8192], P('tau', 'row', 'col'), may hold values from -6 to 6
- virtual_green: bfloat16 [8, 8192, 2048], P('tau', 'row', 'col'), may hold values from -0.0625 to 0.0625
- occ_mask: int32 [8, 64], P('row', 'col'), may hold values 0 or 1
- virt_mask: int32 [64, 16], P('row', 'col'), may hold values 0 or 1
- chi_mask: int32 [8, 16], P('row', 'col'), may hold values 0 or 1
- cosine_weights: float32 [8, 8], replicated, may hold values from -3 to 3
Outputs:
- chi_freq: float32 [8, 1024, 2048], P(None, ('row', 'tau'), 'col')
All inputs are finite; a program needn't handle non-finite values. No bound on the sum of `occ_mask` or of `virt_mask` or of `chi_mask` on one device may be relied on, other than what follows from the above.
Results may differ from a plain program's by a relative error of at most 0.0029.
Values may be sent and summed in bfloat16 or wider, within the bound.
A program may use at most 64 MiB of HBM per device.

v0:
```python
import jax
import jax.numpy as jnp
from jax import lax
from jax.sharding import PartitionSpec as P


def copy_for_each(value, axis):
    count = lax.axis_size(axis)
    return lax.all_to_all(
        jnp.broadcast_to(value[None], (count, *value.shape)), axis, 0, 0, tiled=True
    )


def joined_along(blocks, dim):
    shape = list(blocks.shape[1:])
    shape[dim] *= blocks.shape[0]
    return jnp.moveaxis(blocks, 0, dim).reshape(shape)


def collect(value, axis, dim):
    blocks = copy_for_each(value, axis)
    return joined_along(blocks, dim)


def expand_mask(values, flags):
    block_rows = values.shape[0] // flags.shape[0]
    block_cols = values.shape[1] // flags.shape[1]
    shaped = values.reshape(flags.shape[0], block_rows, flags.shape[1], block_cols)
    masked = shaped * flags.astype(values.dtype)[:, None, :, None]
    return masked.reshape(values.shape)


def shards(occupied, virtual_green, occ_mask, virt_mask, chi_mask, cosine_weights):
    occ_tile = expand_mask(occupied[0], occ_mask)
    virt_tile = expand_mask(virtual_green[0], virt_mask)
    virt_column = lax.all_gather(virt_tile, "row", axis=0, tiled=True)
    accumulated = jnp.dot(
        collect(occ_tile, "col", 1), virt_column, preferred_element_type=jnp.float32
    )
    chi_local = expand_mask(accumulated, chi_mask).astype(jnp.bfloat16)
    regrouped = lax.all_to_all(chi_local[None], "tau", split_axis=1, concat_axis=0, tiled=True)
    return jnp.einsum(
        "kt,tij->kij",
        cosine_weights,
        regrouped.astype(jnp.float32),
        precision=lax.Precision.HIGHEST,
    )


def solution(mesh):
    placed = (
        P("tau", "row", "col"),
        P("tau", "row", "col"),
        P("row", "col"),
        P("row", "col"),
        P("row", "col"),
        P(),
    )
    return jax.shard_map(
        shards,
        mesh=mesh,
        in_specs=placed,
        out_specs=P(None, ("row", "tau"), "col"),
        check_vma=False,
    )
```

profile of v0, /device:TPU:24, one launch (start us, length us, event | category | flops | bytes accessed | tf_op | source)
XLA Modules:
  0.0 165.8 jit_solution(2362016631813210816)
XLA Ops:
  6.5 0.0 copy-start
  6.5 0.0 copy-start.2
  6.5 0.0 copy-start.1
  6.5 0.0 all-gather.2.cloned.1.call-start
  6.5 0.7 convert_element_type.24
  7.3 0.1 copy.16
  7.4 0.3 mul.44
  7.7 1.9 %bitcast_multiply_fusion = bf16[1024,256]{1,0:T(8,128)(2,1)} fusion(bf16[128,8,2,128]{3,2,1,0:T(2,128)(2,1)S(1)} %bitcast.31, bf16[1,1024,256]{2,1,0:T(8,128)(2,1)} %param.7), kind=kLoop, calls=%fused_computation.3 | loop fusion | flops 262144 | bytes 1572864 | tf_op jit(solution)/shard_map/mul | solution.py:29
  9.6 0.0 all-gather.2.cloned.1.call-update
  9.7 0.0 copy-done.2
  9.7 0.1 broadcast_bitcast_fusion
  9.8 0.0 copy-done.1
  9.8 1.6 broadcast_in_dim.5
  11.4 0.0 copy-start.3
  11.4 17.7 %all-to-all-start = ((bf16[8,128,1024]{2,1,0:T(8,128)(2,1)}), bf16[8,128,1024]{2,1,0:T(8,128)(2,1)S(1)}, u32[]{:S(2)}, u32[]{:S(2)}) async-start(bf16[8,128,1024]{2,1,0:T(8,128)(2,1)} %broadcast_in_dim.5), calls=%async_computation | async-start | bytes 4194304 | tf_op jit(solution)/shard_map/all_to_all | solution.py:9
  29.1 0.0 copy-done.3
  29.1 22.7 %all-gather.2.cloned.1.call-done = bf16[8192,256]{1,0:T(8,128)(2,1)} async-done(((bf16[1024,256]{1,0:T(8,128)(2,1)}), bf16[8192,256]{1,0:T(8,128)(2,1)}) %all-gather.2.cloned.1.call-update) | async-done | bytes 4194320 | tf_op jit(solution)/shard_map/all_gather | solution.py:36
  51.9 6.4 %copy.17 = bf16[256,8192]{1,0:T(8,128)(2,1)} copy(bf16[256,8192]{0,1:T(8,128)(2,1)} %bitcast.30) | data formatting | bytes 8388608 | tf_op jit(solution)/shard_map/dot_general | solution.py:37
  58.3 20.7 %all-to-all-done = bf16[8,128,1024]{2,1,0:T(8,128)(2,1)S(1)} async-done(((bf16[8,128,1024]{2,1,0:T(8,128)(2,1)}), bf16[8,128,1024]{2,1,0:T(8,128)(2,1)S(1)}, u32[]{:S(2)}, u32[]{:S(2)}) %all-to-all-start) | async-done | bytes 2097184 | tf_op jit(solution)/shard_map/all_to_all | solution.py:9
  79.0 2.5 %copy.15 = bf16[128,8,1024]{2,1,0:T(8,128)(2,1)} copy(bf16[128,8,1024]{2,0,1:T(8,128)(2,1)S(1)} %bitcast.29) | data formatting | bytes 4194304 | tf_op jit(solution)/shard_map/transpose | solution.py:17
  81.5 2.9 %reshape.38 = bf16[128,8192,1]{1,0,2:T(8,128)(2,1)S(1)} reshape(bf16[128,8,1024]{2,1,0:T(8,128)(2,1)} %copy.15) | data formatting | bytes 4194304 | tf_op jit(solution)/shard_map/reshape | solution.py:17
  84.3 3.4 %fusion = bf16[128,2,128]{0,2,1:T(8,128)(2,1)S(1)} fusion(bf16[128,8192,1]{1,0,2:T(8,128)(2,1)S(1)} %reshape.38, bf16[2,128,8192]{2,1,0:T(8,128)(2,1)} %bitcast.28, f32[2]{0:T(128)S(1)} %convert_bitcast_fusion), kind=kOutput, calls=%fused_computation.2 | convolution fusion | flops 536936448 | bytes 6357000 | tf_op jit(solution)/shard_map/dot_general | solution.py:37
  87.8 0.1 copy.18
  87.9 0.5 broadcast.9
  88.4 1.0 reduce
  89.5 68.5 %all_to_all.17 = bf16[8,2,2048]{2,1,0:T(2,128)(2,1)S(1)} all-to-all(bf16[8,2,2048]{2,1,0:T(2,128)(2,1)S(1)} %reshape.41), channel_id=1, replica_groups=mesh['tau'=8,'row'=8,'col'=8] {'tau'}, dimensions={0} | all-to-all | bytes 131072 | tf_op jit(solution)/shard_map/all_to_all | solution.py:41
  158.0 0.1 reshape.42
  158.1 0.0 copy-done
  158.1 0.2 convolution_bitcast_fusion
  158.3 0.7 copy.20
  (5 shorter events, 0.1 us)
Async XLA Ops:
  6.5 151.6 %copy-start = (f32[8,8]{1,0:T(8,128)S(1)}, f32[8,8]{1,0:T(8,128)}, u32[]{:S(2)}) copy-start(f32[8,8]{1,0:T(8,128)} %param.11) | copy-start | bytes 772
  6.5 3.1 %copy-start.2 = (s32[1,8]{1,0:T(1,128)S(1)}, s32[1,8]{1,0:T(1,128)}, u32[]{:S(2)}) copy-start(s32[1,8]{1,0:T(1,128)} %param.8) | copy-start | bytes 100
  6.5 3.2 %copy-start.1 = (bf16[1,128,1024]{2,1,0:T(8,128)(2,1)S(1)}, bf16[1,128,1024]{2,1,0:T(8,128)(2,1)}, u32[]{:S(2)}) copy-start(bf16[1,128,1024]{2,1,0:T(8,128)(2,1)} %param.6) | copy-start | bytes 786436
  6.5 45.3 %all-gather.2.cloned.1.call-start = ((), (), s32[]{:S(2)}) async-start(), calls=%async_computation.2 | async-start | bytes 4718592 | tf_op jit(solution)/shard_map/all_gather | solution.py:36
  11.4 17.7 %copy-start.3 = (s32[1,2]{1,0:T(1,128)S(1)}, s32[1,2]{1,0:T(1,128)}, u32[]{:S(2)}) copy-start(s32[1,2]{1,0:T(1,128)} %param.10) | copy-start | bytes 28
  11.4 67.6 %all-to-all-start = ((bf16[8,128,1024]{2,1,0:T(8,128)(2,1)}), bf16[8,128,1024]{2,1,0:T(8,128)(2,1)S(1)}, u32[]{:S(2)}, u32[]{:S(2)}) async-start(bf16[8,128,1024]{2,1,0:T(8,128)(2,1)} %broadcast_in_dim.5), calls=%async_computation | async-start | bytes 4194304 | tf_op jit(solution)/shard_map/all_to_all | solution.py:9
Sparse Core Ops, SparseCore 0:
  9.8 42.0 all-gather.1
where the time goes:
time: 166 us
  blocking collectives  68.5 us (41%)
  waiting for transfers between devices  43.5 us (26%)
  starting transfers between devices  17.7 us (11%)
  local copies, waits for them, and re-layouts  15.3 us (9%)
  between operations  13.5 us (8%)
  other arithmetic  3.7 us (2%)
  matrix products  3.64 us (2%)
    all_to_all x1, blocking collectives, shards(): lax.all_to_all(chi_local[None], 'tau', split_axis=1, concat_axis=0, tiled...  68.5 us
    all_gather x1, waiting for transfers between devices, shards(): virt_column = lax.all_gather(virt_tile, 'row', axis=0, tiled=True)  22.7 us
    all_to_all x1, waiting for transfers between devices, copy_for_each(): lax.all_to_all(jnp.broadcast_to(value[None], (count, *value.shape)), axis...  20.7 us
    all_to_all x1, starting transfers between devices, copy_for_each(): lax.all_to_all(jnp.broadcast_to(value[None], (count, *value.shape)), axis...  17.7 us
    dot_general x1, local copies, waits for them, and re-layouts, shards(): jnp.dot(collect(occ_tile, 'col', 1), virt_column, preferred_element_type=...  6.39 us
    dot_general x1, matrix products, shards(): jnp.dot(collect(occ_tile, 'col', 1), virt_column, preferred_element_type=...  3.45 us
  transfers between devices with their start and end apart: 2, of which 2 were waited for; matrix products, arithmetic and copies ran while one was open for 5% of the time, Pallas kernels for 0%

commit v1 on v0

v1 whole, which is shorter than its diff:
```python
import functools

import jax
import jax.numpy as jnp
from jax import lax
from jax.experimental import pallas as pl
from jax.experimental.pallas import tpu as pltpu
from jax.sharding import PartitionSpec as P

MESH = pl.DeviceIdType.MESH
CH = 8
OFFS = (1, 3, 2)


def kernel(
    occ_hbm, virt_hbm, occ_mask, virt_mask, chi_mask, weights, out_ref,
    occ, virt, acc, chi, regroup,
    load_sem, z_sem, x_sem, xc_sem, y_sem, d_sem, t_sem, right_sem, left_sem,
):
    tau = lax.axis_index("tau")
    row = lax.axis_index("row")
    col = lax.axis_index("col")
    y, core = row // 2, lax.rem(row, 2)
    x, half = col // 2, lax.rem(col, 2)
    mine = col
    cross = x * 2 + 1 - half

    def x_peer(o):
        return (tau, row, lax.rem(x + o, 4) * 2 + half)

    def y_peer(o):
        return (tau, lax.rem(y + o, 4) * 2 + core, col)

    partner = (tau, y * 2 + 1 - core, col)
    across = (tau, row, cross)

    loads = [
        pltpu.make_async_copy(
            occ_hbm.at[0, :, pl.ds(c * 128, 128)], occ.at[mine, c], load_sem.at[c]
        )
        for c in range(CH)
    ]
    loads.append(pltpu.make_async_copy(virt_hbm.at[0], virt.at[row], load_sem.at[CH]))
    for load in loads:
        load.start()

    barrier = pltpu.get_barrier_semaphore()
    for peer in [x_peer(o) for o in OFFS] + [y_peer(o) for o in OFFS] + [partner, across]:
        pl.semaphore_signal(barrier, inc=1, device_id=peer, device_id_type=MESH)

    @pl.when(tau < 7)
    def _():
        pl.semaphore_signal(barrier, inc=1, device_id=(tau + 1, row, col), device_id_type=MESH)

    @pl.when(tau > 0)
    def _():
        pl.semaphore_signal(barrier, inc=1, device_id=(tau - 1, row, col), device_id_type=MESH)

    for c in range(CH):
        loads[c].wait()
        flag = occ_mask[0, c].astype(jnp.float32)
        occ[mine, c] = (occ[mine, c].astype(jnp.float32) * flag).astype(jnp.bfloat16)
    loads[CH].wait()
    for i in range(8):
        for j in range(2):
            flag = virt_mask[i, j].astype(jnp.float32)
            block = virt[row, pl.ds(i * 128, 128), pl.ds(j * 128, 128)]
            virt[row, pl.ds(i * 128, 128), pl.ds(j * 128, 128)] = (
                block.astype(jnp.float32) * flag
            ).astype(jnp.bfloat16)

    ends = jnp.where(tau == 0, 1, 0) + jnp.where(tau == 7, 1, 0)
    pl.semaphore_wait(barrier, 10 - ends)

    def remote(src, dst, sems, at, peer):
        return pltpu.make_async_remote_copy(
            src_ref=src, dst_ref=dst, send_sem=sems.at[(0, *at)], recv_sem=sems.at[(1, *at)],
            device_id=peer, device_id_type=MESH,
        )

    def z_copy(c):
        return remote(occ.at[mine, c], occ.at[mine, c], z_sem, (c,), across)

    def x_copy(i):
        return remote(occ.at[mine], occ.at[mine], x_sem, (i,), x_peer(OFFS[i]))

    def xc_copy(c, i):
        return remote(occ.at[cross, c], occ.at[cross, c], xc_sem, (c, i), x_peer(OFFS[i]))

    def y_copy(i):
        return remote(virt.at[row], virt.at[row], y_sem, (i,), y_peer(OFFS[i]))

    def d_copy(i):
        r = row if i == 0 else lax.rem(y + 4 - OFFS[i - 1], 4) * 2 + core
        return remote(virt.at[r], virt.at[r], d_sem, (i,), partner)

    def t_copy(o):
        to = lax.rem(tau + o, 8)
        return remote(chi.at[to], regroup.at[tau], t_sem, (o - 1,), (to, row, col))

    for c in range(CH):
        z_copy(c).start()
    for i in range(3):
        x_copy(i).start()
        y_copy(i).start()
        if i == 0:
            d_copy(0).start()

    @pl.when(tau > 0)
    def _():
        pl.semaphore_wait(right_sem, 1)

    @pl.when(tau < 7)
    def _():
        pl.semaphore_signal(right_sem, inc=1, device_id=(tau + 1, row, col), device_id_type=MESH)
        pl.semaphore_wait(left_sem, 1)

    @pl.when(tau > 0)
    def _():
        pl.semaphore_signal(left_sem, inc=1, device_id=(tau - 1, row, col), device_id_type=MESH)

    def dot_chunks(kb, first, count):
        total = None
        for c in range(first, first + count, 2):
            lhs = jnp.concatenate([occ[kb, c], occ[kb, c + 1]], axis=1)
            rhs = virt[kb, pl.ds(c * 128, 256), :]
            part = jnp.dot(lhs, rhs, preferred_element_type=jnp.float32)
            total = part if total is None else total + part
        return total

    def block_of(o, h):
        return lax.rem(y + 4 - o, 4) * 2 + h

    def own_half(o):
        acc[...] += dot_chunks(block_of(o, half), 0, CH)

    def cross_half(o, first, count):
        acc[...] += dot_chunks(block_of(o, 1 - half), first, count)

    def z_arrived(c):
        z_copy(c).wait_recv()
        for i in range(3):
            xc_copy(c, i).start()

    def y_arrived(i):
        y_copy(i).wait_recv()
        d_copy(i + 1).start()

    def xc_arrived(c):
        for i in range(3):
            xc_copy(c, i).wait_recv()

    acc[...] = jnp.zeros_like(acc)
    z_arrived(0)
    z_arrived(1)
    z_arrived(2)
    d_copy(0).wait_recv()
    for i in range(3):
        x_copy(i).wait_recv()
    own_half(0)
    y_arrived(0)
    y_arrived(1)
    z_arrived(3)
    d_copy(1).wait_recv()
    own_half(1)
    d_copy(2).wait_recv()
    own_half(3)
    z_arrived(4)
    for pair in (0, 2):
        xc_arrived(pair)
        xc_arrived(pair + 1)
        for o in (0, 1, 3):
            cross_half(o, pair, 2)
    z_arrived(5)
    z_arrived(6)
    z_arrived(7)
    y_arrived(2)
    xc_arrived(4)
    xc_arrived(5)
    for o in (0, 1, 3):
        cross_half(o, 4, 2)
    d_copy(3).wait_recv()
    own_half(2)
    cross_half(2, 0, 6)
    xc_arrived(6)
    xc_arrived(7)
    for o in (0, 1, 3, 2):
        cross_half(o, 6, 2)

    for j in range(2):
        flag = chi_mask[0, j].astype(jnp.float32)
        cols = pl.ds(j * 128, 128)
        chi[:, :, cols] = (acc[:, cols] * flag).astype(jnp.bfloat16).reshape(8, 16, 128)
    for o in (4, 5, 3, 6, 2, 7, 1):
        t_copy(o).start()
    regroup[tau] = chi[tau]
    for o in (1, 7, 2, 6, 3, 5, 4):
        t_copy(o).wait_recv()
    slices = [regroup[t].astype(jnp.float32) for t in range(8)]
    for k in range(8):
        total = slices[0] * weights[k, 0]
        for t in range(1, 8):
            total = total + slices[t] * weights[k, t]
        out_ref[k] = total

    for c in range(CH):
        z_copy(c).wait_send()
        for i in range(3):
            xc_copy(c, i).wait_send()
    for i in range(3):
        x_copy(i).wait_send()
        y_copy(i).wait_send()
    for i in range(4):
        d_copy(i).wait_send()
    for o in range(1, 8):
        t_copy(o).wait_send()


def shards(occupied, virtual_green, occ_mask, virt_mask, chi_mask, cosine_weights):
    smem = pl.BlockSpec(memory_space=pltpu.SMEM)
    hbm = pl.BlockSpec(memory_space=pl.ANY)
    dma = pltpu.SemaphoreType.DMA
    return pl.pallas_call(
        kernel,
        out_shape=jax.ShapeDtypeStruct((8, 16, 256), jnp.float32),
        in_specs=[hbm, hbm, smem, smem, smem, smem],
        out_specs=pl.BlockSpec(memory_space=pltpu.VMEM),
        scratch_shapes=[
            pltpu.VMEM((8, CH, 128, 128), jnp.bfloat16),
            pltpu.VMEM((8, 1024, 256), jnp.bfloat16),
            pltpu.VMEM((128, 256), jnp.float32),
            pltpu.VMEM((8, 16, 256), jnp.bfloat16),
            pltpu.VMEM((8, 16, 256), jnp.bfloat16),
            dma((CH + 1,)),
            dma((2, CH)),
            dma((2, 3)),
            dma((2, CH, 3)),
            dma((2, 3)),
            dma((2, 4)),
            dma((2, 7)),
            pltpu.SemaphoreType.REGULAR,
            pltpu.SemaphoreType.REGULAR,
        ],
        compiler_params=pltpu.CompilerParams(collective_id=0, has_side_effects=True),
        name="polarizability",
    )(occupied, virtual_green, occ_mask, virt_mask, chi_mask, cosine_weights)


def solution(mesh):
    placed = (
        P("tau", "row", "col"),
        P("tau", "row", "col"),
        P("row", "col"),
        P("row", "col"),
        P("row", "col"),
        P(),
    )
    return jax.shard_map(
        shards,
        mesh=mesh,
        in_specs=placed,
        out_specs=P(None, ("row", "tau"), "col"),
        check_vma=False,
    )
```

time: 166 us -> 61.5 us (0.37)
  blocking collectives: 68.5 us -> 0 us
  Pallas kernels: 0 us -> 57.8 us
  waiting for transfers between devices: 43.5 us -> 0 us
  starting transfers between devices: 17.7 us -> 0 us
  between operations: 13.5 us -> 0.01 us
  local copies, waits for them, and re-layouts: 15.3 us -> 2.91 us
  other arithmetic: 3.7 us -> 0 us
  matrix products: 3.64 us -> 0 us
    all_to_all x1 -> x0, blocking collectives: 68.5 us -> none  [shards(): lax.all_to_all(chi_local[None], 'tau', split_axis=1, concat_axis=0, tiled...]
    pallas_call x0 -> x1, Pallas kernels: none -> 57.8 us  [shards(): pl.pallas_call(kernel, out_shape=jax.ShapeDtypeStruct((8, 16, 256), jnp.f...]
    all_gather x1 -> x0, waiting for transfers between devices: 22.7 us -> none  [shards(): virt_column = lax.all_gather(virt_tile, 'row', axis=0, tiled=True)]
    all_to_all x1 -> x0, waiting for transfers between devices: 20.7 us -> none  [copy_for_each(): lax.all_to_all(jnp.broadcast_to(value[None], (count, *value.shape)), axis...]
    all_to_all x1 -> x0, starting transfers between devices: 17.7 us -> none  [copy_for_each(): lax.all_to_all(jnp.broadcast_to(value[None], (count, *value.shape)), axis...]
    dot_general x2 -> x0, local copies, waits for them, and re-layouts: 7.09 us -> none  [the longest x1 6.39 us: shards(): jnp.dot(collect(occ_tile, 'col', 1), virt_column, preferred_element_type=...]
    dot_general x2 -> x0, matrix products: 3.64 us -> none  [the longest x1 3.45 us: shards(): jnp.dot(collect(occ_tile, 'col', 1), virt_column, preferred_element_type=...]
    reshape x1 -> x0, local copies, waits for them, and re-layouts: 2.87 us -> none  [joined_along(): return jnp.moveaxis(blocks, 0, dim).reshape(shape)]
  transfers between devices with their start and end apart: 2 -> 0, of which waited for: 2 -> 0; matrix products, arithmetic and copies ran while one was open for 5% -> 0% of each run, Pallas kernels for 0% -> 0%
where the time goes in v1:
time: 61.5 us; the launch traced here: 60.7 us
  Pallas kernels  57.8 us (94%)
  local copies, waits for them, and re-layouts  2.91 us (5%)
    pallas_call x1, Pallas kernels, shards(): pl.pallas_call(kernel, out_shape=jax.ShapeDtypeStruct((8, 16, 256), jnp.f...  57.8 us
    unnamed x2, local copies, waits for them, and re-layouts  2.91 us

profile of v1, /device:TPU:24, one launch (start us, length us, event | category | flops | bytes accessed | tf_op | source)
XLA Modules:
  0.0 60.7 jit_solution(3572495259079275570)
XLA Ops:
  0.0 1.3 %copy.7.virt_mask = s32[8,2]{1,0:T(8,128)} copy(s32[8,2]{0,1:T(2,128)} %param.9) | data formatting | bytes 128 | tf_op args[3]
  1.3 57.8 %polarizability.1 = f32[8,16,256]{2,1,0:T(8,128)} custom-call(bf16[1,128,1024]{2,1,0:T(8,128)(2,1)} %occ_hbm.1, bf16[1,1024,256]{2,1,0:T(8,128)(2,1)} %virt_hbm.1, s32[1,8]{1,0:T(1,128)} %occ_mask.1, s32[8,2]{1,0:T(8,128)} %copy.7.virt_mask, s32[1,2]{1,0:T(1,128)} %chi_mask.1, f32[8,8]{1,0:T(8,128)} %weights.1), custom_call_target="tpu_custom_call" | custom-call | tf_op jit(solution)/shard_map/polarizability/pallas_call | solution.py:223
  59.2 1.6 %copy.9 = f32[8,16,256]{2,1,0:T(8,128)} copy(f32[8,16,256]{2,1,0:T(8,128)} %polarizability.1) | data formatting | bytes 262144

commit v2 on v1

v2 whole, which is shorter than its diff:
```python
import functools

import jax
import jax.numpy as jnp
from jax import lax
from jax.experimental import pallas as pl
from jax.experimental.pallas import tpu as pltpu
from jax.sharding import PartitionSpec as P

MESH = pl.DeviceIdType.MESH
CH = 8
OFFS = (2, 1, 3)


def kernel(
    occ_hbm, virt_hbm, occ_mask_hbm, virt_mask_hbm, chi_mask_hbm, weights_hbm, out_ref,
    occ, virt, acc, chi, regroup, occ_mask, virt_mask, chi_mask, weights,
    load_sem, z_sem, x_sem, xc_sem, y_sem, d_sem, own_sem, t_sem, reach_sem,
):
    tau = lax.axis_index("tau")
    row = lax.axis_index("row")
    col = lax.axis_index("col")
    y, core = row // 2, lax.rem(row, 2)
    x, half = col // 2, lax.rem(col, 2)
    mine = col
    cross = x * 2 + 1 - half

    def x_peer(o):
        return (tau, row, lax.rem(x + o, 4) * 2 + half)

    def y_peer(o):
        return (tau, lax.rem(y + o, 4) * 2 + core, col)

    partner = (tau, y * 2 + 1 - core, col)
    across = (tau, row, cross)

    barrier = pltpu.get_barrier_semaphore()
    for peer in [x_peer(o) for o in OFFS] + [y_peer(1), y_peer(3), partner, across]:
        pl.semaphore_signal(barrier, inc=1, device_id=peer, device_id_type=MESH)

    @pl.when(tau < 7)
    def _():
        pl.semaphore_signal(barrier, inc=1, device_id=(tau + 1, row, col), device_id_type=MESH)

    @pl.when(tau > 0)
    def _():
        pl.semaphore_signal(barrier, inc=1, device_id=(tau - 1, row, col), device_id_type=MESH)

    loads = [
        pltpu.make_async_copy(
            occ_hbm.at[0, :, pl.ds(c * 128, 128)], occ.at[mine, c], load_sem.at[c]
        )
        for c in range(CH)
    ]
    loads.append(pltpu.make_async_copy(virt_hbm.at[0], virt.at[row], load_sem.at[CH]))
    small = [
        pltpu.make_async_copy(src, dst, load_sem.at[CH + 1 + i])
        for i, (src, dst) in enumerate(
            [
                (occ_mask_hbm, occ_mask),
                (virt_mask_hbm, virt_mask),
                (chi_mask_hbm, chi_mask),
                (weights_hbm, weights),
            ]
        )
    ]
    small[0].start()
    for load in loads:
        load.start()
    for load in small[1:]:
        load.start()

    small[0].wait()
    for c in range(CH):
        loads[c].wait()
        flag = occ_mask[0, c].astype(jnp.float32)
        occ[mine, c] = (occ[mine, c].astype(jnp.float32) * flag).astype(jnp.bfloat16)
    ends = jnp.where(tau == 0, 1, 0) + jnp.where(tau == 7, 1, 0)
    pl.semaphore_wait(barrier, 9 - ends)

    def remote(src, dst, sems, at, peer):
        return pltpu.make_async_remote_copy(
            src_ref=src, dst_ref=dst, send_sem=sems.at[(0, *at)], recv_sem=sems.at[(1, *at)],
            device_id=peer, device_id_type=MESH,
        )

    def z_copy(c):
        return remote(occ.at[mine, c], occ.at[mine, c], z_sem, (c,), across)

    def x_copy(i):
        return remote(occ.at[mine], occ.at[mine], x_sem, (i,), x_peer(OFFS[i]))

    def xc_copy(c, i):
        return remote(occ.at[cross, c], occ.at[cross, c], xc_sem, (c, i), x_peer(OFFS[i]))

    def quarter(r, way, k):
        return virt.at[r, pl.ds(512 * ((way + k // 2) % 2) + 256 * (k % 2), 256)]

    def y_copy(way, k):
        r = row if k < 4 else lax.rem(y + 3 - 2 * way, 4) * 2 + core
        part = quarter(r, way, k)
        return remote(part, part, y_sem, (way, k), y_peer(1 + 2 * way))

    def d_copy(way, k):
        r = lax.rem(y + (3 - 2 * way if k < 4 else 2), 4) * 2 + core
        part = quarter(r, way, k)
        return remote(part, part, d_sem, (way, k), partner)

    def own_copy():
        return remote(virt.at[row], virt.at[row], own_sem, (), partner)

    def t_copy(o):
        to = lax.rem(tau + o, 8)
        return remote(chi.at[to], regroup.at[tau], t_sem, (o - 1,), (to, row, col))

    for c in range(2):
        z_copy(c).start()
    for i in range(3):
        x_copy(i).start()
    loads[CH].wait()
    small[1].wait()
    for i in range(8):
        for j in range(2):
            flag = virt_mask[j, i].astype(jnp.float32)
            block = virt[row, pl.ds(i * 128, 128), pl.ds(j * 128, 128)]
            virt[row, pl.ds(i * 128, 128), pl.ds(j * 128, 128)] = (
                block.astype(jnp.float32) * flag
            ).astype(jnp.bfloat16)

    for k in range(4):
        for way in range(2):
            y_copy(way, k).start()
    own_copy().start()
    small[2].wait()
    small[3].wait()

    def tell(k):
        for step in (-(2**k), 2**k):
            @pl.when(jnp.logical_and(tau + step >= 0, tau + step < 8))
            def _():
                pl.semaphore_signal(
                    reach_sem.at[k], inc=1, device_id=(tau + step, row, col), device_id_type=MESH
                )

    def hear(k):
        below, above = jnp.where(tau >= 2**k, 1, 0), jnp.where(tau < 8 - 2**k, 1, 0)
        pl.semaphore_wait(reach_sem.at[k], below + above)

    tell(0)

    def dot_chunks(kb, first, count):
        total = None
        for c in range(first, first + count, 2):
            lhs = jnp.concatenate([occ[kb, c], occ[kb, c + 1]], axis=1)
            rhs = virt[kb, pl.ds(c * 128, 256), :]
            part = jnp.dot(lhs, rhs, preferred_element_type=jnp.float32)
            total = part if total is None else total + part
        return total

    def block_of(o, h):
        return lax.rem(y + 4 - o, 4) * 2 + h

    def own_half(o):
        acc[...] += dot_chunks(block_of(o, half), 0, CH)

    def cross_half(o, first, count):
        acc[...] += dot_chunks(block_of(o, 1 - half), first, count)

    def z_arrived(c):
        z_copy(c).wait_recv()
        for i in range(3):
            xc_copy(c, i).start()

    def y_arrived(k):
        for way in range(2):
            y_copy(way, k).wait_recv()
            if k < 2:
                y_copy(way, k + 4).start()
            d_copy(way, k).start()
        z_copy(k + 2).start()

    def d_arrived(k):
        for way in range(2):
            d_copy(way, k).wait_recv()

    def xc_arrived(c):
        for i in range(3):
            xc_copy(c, i).wait_recv()

    acc[...] = jnp.zeros_like(acc)
    y_arrived(0)
    y_arrived(1)
    hear(0)
    tell(1)
    y_arrived(2)
    z_arrived(0)
    y_arrived(3)
    z_arrived(1)
    y_arrived(4)
    z_arrived(2)
    y_arrived(5)
    hear(1)
    tell(2)
    z_arrived(3)
    own_copy().wait_recv()
    for i in range(3):
        x_copy(i).wait_recv()
    own_half(0)
    z_arrived(4)
    for k in range(4):
        d_arrived(k)
    own_half(1)
    own_half(3)
    z_arrived(5)
    d_arrived(4)
    d_arrived(5)
    own_half(2)
    hear(2)
    z_arrived(6)
    for pair in (0, 2):
        xc_arrived(pair)
        xc_arrived(pair + 1)
        for o in range(4):
            cross_half(o, pair, 2)
    z_arrived(7)
    for pair in (4, 6):
        xc_arrived(pair)
        xc_arrived(pair + 1)
        for o in range(4):
            cross_half(o, pair, 2)

    for j in range(2):
        flag = chi_mask[0, j].astype(jnp.float32)
        cols = pl.ds(j * 128, 128)
        chi[:, :, cols] = (acc[:, cols] * flag).astype(jnp.bfloat16).reshape(8, 16, 128)
    for o in (4, 5, 3, 6, 2, 7, 1):
        t_copy(o).start()
    regroup[tau] = chi[tau]
    for o in (1, 7, 2, 6, 3, 5, 4):
        t_copy(o).wait_recv()
    slices = [regroup[t].astype(jnp.float32) for t in range(8)]
    for k in range(8):
        total = slices[0] * weights[k, 0]
        for t in range(1, 8):
            total = total + slices[t] * weights[k, t]
        out_ref[k] = total

    for c in range(CH):
        z_copy(c).wait_send()
        for i in range(3):
            xc_copy(c, i).wait_send()
    for i in range(3):
        x_copy(i).wait_send()
    for k in range(6):
        for way in range(2):
            y_copy(way, k).wait_send()
            d_copy(way, k).wait_send()
    own_copy().wait_send()
    for o in range(1, 8):
        t_copy(o).wait_send()


def shards(occupied, virtual_green, occ_mask, virt_mask, chi_mask, cosine_weights):
    dma = pltpu.SemaphoreType.DMA
    return pl.pallas_call(
        kernel,
        out_shape=jax.ShapeDtypeStruct((8, 16, 256), jnp.float32),
        in_specs=[pl.BlockSpec(memory_space=pl.ANY)] * 6,
        out_specs=pl.BlockSpec(memory_space=pltpu.VMEM),
        scratch_shapes=[
            pltpu.VMEM((8, CH, 128, 128), jnp.bfloat16),
            pltpu.VMEM((8, 1024, 256), jnp.bfloat16),
            pltpu.VMEM((128, 256), jnp.float32),
            pltpu.VMEM((8, 16, 256), jnp.bfloat16),
            pltpu.VMEM((8, 16, 256), jnp.bfloat16),
            pltpu.SMEM((1, 8), jnp.int32),
            pltpu.SMEM((2, 8), jnp.int32),
            pltpu.SMEM((1, 2), jnp.int32),
            pltpu.SMEM((8, 8), jnp.float32),
            dma((CH + 5,)),
            dma((2, CH)),
            dma((2, 3)),
            dma((2, CH, 3)),
            dma((2, 2, 6)),
            dma((2, 2, 6)),
            dma((2,)),
            dma((2, 7)),
            pltpu.SemaphoreType.REGULAR((3,)),
        ],
        compiler_params=pltpu.CompilerParams(collective_id=0, has_side_effects=True),
        name="polarizability",
    )(occupied, virtual_green, occ_mask, virt_mask.T, chi_mask, cosine_weights)


def solution(mesh):
    placed = (
        P("tau", "row", "col"),
        P("tau", "row", "col"),
        P("row", "col"),
        P("row", "col"),
        P("row", "col"),
        P(),
    )
    return jax.shard_map(
        shards,
        mesh=mesh,
        in_specs=placed,
        out_specs=P(None, ("row", "tau"), "col"),
        check_vma=False,
    )
```

time: 61.5 us -> 57.9 us (0.941)
  Pallas kernels: 57.8 us -> 55.7 us
  local copies, waits for them, and re-layouts: 2.91 us -> 1.57 us
    pallas_call x1, Pallas kernels: 57.8 us -> 55.7 us  [shards(): pl.pallas_call(kernel, out_shape=jax.ShapeDtypeStruct((8, 16, 256), jnp.f...]
    unnamed x2 -> x1, local copies, waits for them, and re-layouts: 2.91 us -> 1.57 us
where the time goes in v2:
time: 57.9 us; the launch traced here: 57.3 us
  Pallas kernels  55.7 us (96%)
  local copies, waits for them, and re-layouts  1.57 us (3%)
    pallas_call x1, Pallas kernels, shards(): pl.pallas_call(kernel, out_shape=jax.ShapeDtypeStruct((8, 16, 256), jnp.f...  55.7 us
    unnamed x1, local copies, waits for them, and re-layouts  1.57 us

profile of v2, /device:TPU:24, one launch (start us, length us, event | category | flops | bytes accessed | tf_op | source)
XLA Modules:
  0.0 57.3 jit_solution(18319760950641719749)
XLA Ops:
  0.0 55.7 %polarizability.1 = f32[8,16,256]{2,1,0:T(8,128)} custom-call(bf16[1,128,1024]{2,1,0:T(8,128)(2,1)} %occ_hbm.1, bf16[1,1024,256]{2,1,0:T(8,128)(2,1)} %virt_hbm.1, s32[1,8]{1,0:T(1,128)} %occ_mask_hbm.1, s32[2,8]{1,0:T(2,128)} %bitcast.1, s32[1,2]{1,0:T(1,128)} %chi_mask_hbm.1, f32[8,8]{1,0:T(8,128)} %weights_hbm.1), custom_call_target="tpu_custom_call" | custom-call | tf_op jit(solution)/shard_map/polarizability/pallas_call | solution.py:265
  55.7 1.6 %copy.8 = f32[8,16,256]{2,1,0:T(8,128)} copy(f32[8,16,256]{2,1,0:T(8,128)} %polarizability.1) | data formatting | bytes 262144

commit v3 on v2

--- a/solution.py
+++ b/solution.py
@@ -9,6 +9,8 @@
 
 MESH = pl.DeviceIdType.MESH
 CH = 8
+PIECES = [(c, 0, 128) for c in range(7)] + [(7, 0, 64), (7, 64, 64)]
+AHEAD = (3, 3)
 OFFS = (2, 1, 3)
 
 
@@ -84,14 +86,24 @@
             device_id=peer, device_id_type=MESH,
         )
 
-    def z_copy(c):
-        return remote(occ.at[mine, c], occ.at[mine, c], z_sem, (c,), across)
+    def piece(kb, p):
+        c, first, count = PIECES[p]
+        return occ.at[kb, c, pl.ds(first, count)]
+
+    def z_copy(p):
+        return remote(piece(mine, p), piece(mine, p), z_sem, (p,), across)
+
+    def z_start(half_is, p):
+        if p < len(PIECES):
+            @pl.when(half == half_is)
+            def _():
+                z_copy(p).start()
 
     def x_copy(i):
         return remote(occ.at[mine], occ.at[mine], x_sem, (i,), x_peer(OFFS[i]))
 
-    def xc_copy(c, i):
-        return remote(occ.at[cross, c], occ.at[cross, c], xc_sem, (c, i), x_peer(OFFS[i]))
+    def xc_copy(p, i):
+        return remote(piece(cross, p), piece(cross, p), xc_sem, (p, i), x_peer(OFFS[i]))
 
     def quarter(r, way, k):
         return virt.at[r, pl.ds(512 * ((way + k // 2) % 2) + 256 * (k % 2), 256)]
@@ -109,12 +121,16 @@
     def own_copy():
         return remote(virt.at[row], virt.at[row], own_sem, (), partner)
 
-    def t_copy(o):
-        to = lax.rem(tau + o, 8)
-        return remote(chi.at[to], regroup.at[tau], t_sem, (o - 1,), (to, row, col))
-
-    for c in range(2):
-        z_copy(c).start()
+    def t_copy(to, sender):
+        return pltpu.make_async_remote_copy(
+            src_ref=chi.at[to], dst_ref=regroup.at[tau],
+            send_sem=t_sem.at[0, to], recv_sem=t_sem.at[1, sender],
+            device_id=(to, row, col), device_id_type=MESH,
+        )
+
+    for h in range(2):
+        for p in range(AHEAD[h]):
+            z_start(h, p)
     for i in range(3):
         x_copy(i).start()
     loads[CH].wait()
@@ -177,7 +193,11 @@
             if k < 2:
                 y_copy(way, k + 4).start()
             d_copy(way, k).start()
-        z_copy(k + 2).start()
+        for h in range(2):
+            z_start(h, AHEAD[h] + k)
+            if k == 5:
+                for p in range(AHEAD[h] + 6, len(PIECES)):
+                    z_start(h, p)
 
     def d_arrived(k):
         for way in range(2):
@@ -223,9 +243,12 @@
         for o in range(4):
             cross_half(o, pair, 2)
     z_arrived(7)
+    z_arrived(8)
     for pair in (4, 6):
         xc_arrived(pair)
         xc_arrived(pair + 1)
+        if pair == 6:
+            xc_arrived(8)
         for o in range(4):
             cross_half(o, pair, 2)
 
@@ -233,11 +256,16 @@
         flag = chi_mask[0, j].astype(jnp.float32)
         cols = pl.ds(j * 128, 128)
         chi[:, :, cols] = (acc[:, cols] * flag).astype(jnp.bfloat16).reshape(8, 16, 128)
-    for o in (4, 5, 3, 6, 2, 7, 1):
-        t_copy(o).start()
+    for distance in range(7, 0, -1):
+        for to in (tau + distance, tau - distance):
+            @pl.when(jnp.logical_and(to >= 0, to < 8))
+            def _():
+                t_copy(to, tau).start()
+
     regroup[tau] = chi[tau]
-    for o in (1, 7, 2, 6, 3, 5, 4):
-        t_copy(o).wait_recv()
+    for o in range(1, 8):
+        peer = lax.rem(tau + o, 8)
+        t_copy(peer, peer).wait_recv()
     slices = [regroup[t].astype(jnp.float32) for t in range(8)]
     for k in range(8):
         total = slices[0] * weights[k, 0]
@@ -245,10 +273,10 @@
             total = total + slices[t] * weights[k, t]
         out_ref[k] = total
 
-    for c in range(CH):
-        z_copy(c).wait_send()
+    for p in range(len(PIECES)):
+        z_copy(p).wait_send()
         for i in range(3):
-            xc_copy(c, i).wait_send()
+            xc_copy(p, i).wait_send()
     for i in range(3):
         x_copy(i).wait_send()
     for k in range(6):
@@ -257,7 +285,7 @@
             d_copy(way, k).wait_send()
     own_copy().wait_send()
     for o in range(1, 8):
-        t_copy(o).wait_send()
+        t_copy(lax.rem(tau + o, 8), tau).wait_send()
 
 
 def shards(occupied, virtual_green, occ_mask, virt_mask, chi_mask, cosine_weights):
@@ -278,13 +306,13 @@
             pltpu.SMEM((1, 2), jnp.int32),
             pltpu.SMEM((8, 8), jnp.float32),
             dma((CH + 5,)),
-            dma((2, CH)),
+            dma((2, len(PIECES))),
             dma((2, 3)),
-            dma((2, CH, 3)),
+            dma((2, len(PIECES), 3)),
             dma((2, 2, 6)),
             dma((2, 2, 6)),
             dma((2,)),
-            dma((2, 7)),
+            dma((2, 8)),
             pltpu.SemaphoreType.REGULAR((3,)),
         ],
         compiler_params=pltpu.CompilerParams(collective_id=0, has_side_effects=True),

time: 57.9 us -> 55.8 us (0.964)
  Pallas kernels: 55.7 us -> 54 us
    pallas_call x1, Pallas kernels: 55.7 us -> 54 us  [shards(): pl.pallas_call(kernel, out_shape=jax.ShapeDtypeStruct((8, 16, 256), jnp.f...]
where the time goes in v3:
time: 55.8 us; the launch traced here: 55.6 us
  Pallas kernels  54 us (97%)
  local copies, waits for them, and re-layouts  1.57 us (3%)
    pallas_call x1, Pallas kernels, shards(): pl.pallas_call(kernel, out_shape=jax.ShapeDtypeStruct((8, 16, 256), jnp.f...  54 us
    unnamed x1, local copies, waits for them, and re-layouts  1.57 us

profile of v3, /device:TPU:24, one launch (start us, length us, event | category | flops | bytes accessed | tf_op | source)
XLA Modules:
  0.0 55.6 jit_solution(1889876586377988694)
XLA Ops:
  0.0 54.0 %polarizability.1 = f32[8,16,256]{2,1,0:T(8,128)} custom-call(bf16[1,128,1024]{2,1,0:T(8,128)(2,1)} %occ_hbm.1, bf16[1,1024,256]{2,1,0:T(8,128)(2,1)} %virt_hbm.1, s32[1,8]{1,0:T(1,128)} %occ_mask_hbm.1, s32[2,8]{1,0:T(2,128)} %bitcast.1, s32[1,2]{1,0:T(1,128)} %chi_mask_hbm.1, f32[8,8]{1,0:T(8,128)} %weights_hbm.1), custom_call_target="tpu_custom_call" | custom-call | tf_op jit(solution)/shard_map/polarizability/pallas_call | solution.py:293
  54.0 1.6 %copy.8 = f32[8,16,256]{2,1,0:T(8,128)} copy(f32[8,16,256]{2,1,0:T(8,128)} %polarizability.1) | data formatting | bytes 262144

commit v4 on v2

--- a/solution.py
+++ b/solution.py
@@ -9,6 +9,7 @@
 
 MESH = pl.DeviceIdType.MESH
 CH = 8
+AHEAD = 3
 OFFS = (2, 1, 3)
 
 
@@ -109,11 +110,14 @@
     def own_copy():
         return remote(virt.at[row], virt.at[row], own_sem, (), partner)
 
-    def t_copy(o):
-        to = lax.rem(tau + o, 8)
-        return remote(chi.at[to], regroup.at[tau], t_sem, (o - 1,), (to, row, col))
-
-    for c in range(2):
+    def t_copy(to, sender):
+        return pltpu.make_async_remote_copy(
+            src_ref=chi.at[to], dst_ref=regroup.at[tau],
+            send_sem=t_sem.at[0, to], recv_sem=t_sem.at[1, sender],
+            device_id=(to, row, col), device_id_type=MESH,
+        )
+
+    for c in range(AHEAD):
         z_copy(c).start()
     for i in range(3):
         x_copy(i).start()
@@ -177,7 +181,8 @@
             if k < 2:
                 y_copy(way, k + 4).start()
             d_copy(way, k).start()
-        z_copy(k + 2).start()
+        if k + AHEAD < CH:
+            z_copy(k + AHEAD).start()
 
     def d_arrived(k):
         for way in range(2):
@@ -233,18 +238,13 @@
         flag = chi_mask[0, j].astype(jnp.float32)
         cols = pl.ds(j * 128, 128)
         chi[:, :, cols] = (acc[:, cols] * flag).astype(jnp.bfloat16).reshape(8, 16, 128)
-    for o in (4, 5, 3, 6, 2, 7, 1):
-        t_copy(o).start()
+    for distance in range(7, 0, -1):
+        for to in (tau + distance, tau - distance):
+            @pl.when(jnp.logical_and(to >= 0, to < 8))
+            def _():
+                t_copy(to, tau).start()
+
     regroup[tau] = chi[tau]
-    for o in (1, 7, 2, 6, 3, 5, 4):
-        t_copy(o).wait_recv()
-    slices = [regroup[t].astype(jnp.float32) for t in range(8)]
-    for k in range(8):
-        total = slices[0] * weights[k, 0]
-        for t in range(1, 8):
-            total = total + slices[t] * weights[k, t]
-        out_ref[k] = total
-
     for c in range(CH):
         z_copy(c).wait_send()
         for i in range(3):
@@ -257,14 +257,23 @@
             d_copy(way, k).wait_send()
     own_copy().wait_send()
     for o in range(1, 8):
-        t_copy(o).wait_send()
+        t_copy(lax.rem(tau + o, 8), tau).wait_send()
+    for o in range(1, 8):
+        peer = lax.rem(tau + o, 8)
+        t_copy(peer, peer).wait_recv()
+    slices = [regroup[t].astype(jnp.float32) for t in range(8)]
+    for k in range(8):
+        total = slices[0] * weights[k, 0]
+        for t in range(1, 8):
+            total = total + slices[t] * weights[k, t]
+        out_ref[k] = total
 
 
 def shards(occupied, virtual_green, occ_mask, virt_mask, chi_mask, cosine_weights):
     dma = pltpu.SemaphoreType.DMA
     return pl.pallas_call(
         kernel,
-        out_shape=jax.ShapeDtypeStruct((8, 16, 256), jnp.float32),
+        out_shape=pltpu.VMEM((8, 16, 256), jnp.float32),
         in_specs=[pl.BlockSpec(memory_space=pl.ANY)] * 6,
         out_specs=pl.BlockSpec(memory_space=pltpu.VMEM),
         scratch_shapes=[
@@ -284,7 +293,7 @@
             dma((2, 2, 6)),
             dma((2, 2, 6)),
             dma((2,)),
-            dma((2, 7)),
+            dma((2, 8)),
             pltpu.SemaphoreType.REGULAR((3,)),
         ],
         compiler_params=pltpu.CompilerParams(collective_id=0, has_side_effects=True),

time: 57.9 us -> 53.7 us (0.927)
  Pallas kernels: 55.7 us -> 52.9 us
  local copies, waits for them, and re-layouts: 1.57 us -> 0.66 us
    pallas_call x1, Pallas kernels: 55.7 us -> 52.9 us  [shards(): pl.pallas_call(kernel, out_shape=pltpu.VMEM((8, 16, 256), jnp.float32), i...]
    unnamed x1, local copies, waits for them, and re-layouts: 1.57 us -> 0.66 us
where the time goes in v4:
time: 53.7 us; the launch traced here: 53.6 us
  Pallas kernels  52.9 us (99%)
  local copies, waits for them, and re-layouts  0.66 us (1%)
    pallas_call x1, Pallas kernels, shards(): pl.pallas_call(kernel, out_shape=pltpu.VMEM((8, 16, 256), jnp.float32), i...  52.9 us

profile of v4, /device:TPU:24, one launch (start us, length us, event | category | flops | bytes accessed | tf_op | source)
XLA Modules:
  0.0 53.6 jit_solution(6239786565830164987)
XLA Ops:
  0.0 52.9 %polarizability.1 = f32[8,16,256]{2,1,0:T(8,128)S(1)} custom-call(bf16[1,128,1024]{2,1,0:T(8,128)(2,1)} %occ_hbm.1, bf16[1,1024,256]{2,1,0:T(8,128)(2,1)} %virt_hbm.1, s32[1,8]{1,0:T(1,128)} %occ_mask_hbm.1, s32[2,8]{1,0:T(2,128)} %bitcast.1, s32[1,2]{1,0:T(1,128)} %chi_mask_hbm.1, f32[8,8]{1,0:T(8,128)} %weights_hbm.1), custom_call_target="tpu_custom_call" | custom-call | tf_op jit(solution)/shard_map/polarizability/pallas_call | solution.py:274
  53.0 0.7 %copy.8 = f32[8,16,256]{2,1,0:T(8,128)} copy(f32[8,16,256]{2,1,0:T(8,128)S(1)} %polarizability.1) | data formatting | bytes 262144

commit v5 on v4

--- a/solution.py
+++ b/solution.py
@@ -71,11 +71,14 @@
     for load in small[1:]:
         load.start()
 
-    small[0].wait()
-    for c in range(CH):
+    def masked(c):
         loads[c].wait()
         flag = occ_mask[0, c].astype(jnp.float32)
         occ[mine, c] = (occ[mine, c].astype(jnp.float32) * flag).astype(jnp.bfloat16)
+
+    small[0].wait()
+    for c in range(AHEAD):
+        masked(c)
     ends = jnp.where(tau == 0, 1, 0) + jnp.where(tau == 7, 1, 0)
     pl.semaphore_wait(barrier, 9 - ends)
 
@@ -119,6 +122,8 @@
 
     for c in range(AHEAD):
         z_copy(c).start()
+    for c in range(AHEAD, CH):
+        masked(c)
     for i in range(3):
         x_copy(i).start()
     loads[CH].wait()
@@ -169,6 +174,15 @@
 
     def cross_half(o, first, count):
         acc[...] += dot_chunks(block_of(o, 1 - half), first, count)
+
+    def last_cross(c):
+        total = acc[...]
+        for o in (0, 2):
+            a, b = block_of(o, 1 - half), block_of(o + 1, 1 - half)
+            lhs = jnp.concatenate([occ[a, c], occ[b, c]], axis=1)
+            rhs = jnp.concatenate([virt[r, pl.ds(c * 128, 128), :] for r in (a, b)], axis=0)
+            total += jnp.dot(lhs, rhs, preferred_element_type=jnp.float32)
+        acc[...] = total
 
     def z_arrived(c):
         z_copy(c).wait_recv()
@@ -228,11 +242,13 @@
         for o in range(4):
             cross_half(o, pair, 2)
     z_arrived(7)
-    for pair in (4, 6):
-        xc_arrived(pair)
-        xc_arrived(pair + 1)
-        for o in range(4):
-            cross_half(o, pair, 2)
+    xc_arrived(4)
+    xc_arrived(5)
+    for o in range(4):
+        cross_half(o, 4, 2)
+    for c in (6, 7):
+        xc_arrived(c)
+        last_cross(c)
 
     for j in range(2):
         flag = chi_mask[0, j].astype(jnp.float32)
@@ -258,15 +274,15 @@
     own_copy().wait_send()
     for o in range(1, 8):
         t_copy(lax.rem(tau + o, 8), tau).wait_send()
+    own_slice = regroup[tau].astype(jnp.float32)
+    totals = [own_slice * weights[k, tau] for k in range(8)]
     for o in range(1, 8):
         peer = lax.rem(tau + o, 8)
         t_copy(peer, peer).wait_recv()
-    slices = [regroup[t].astype(jnp.float32) for t in range(8)]
+        arrived = regroup[peer].astype(jnp.float32)
+        totals = [total + arrived * weights[k, peer] for k, total in enumerate(totals)]
     for k in range(8):
-        total = slices[0] * weights[k, 0]
-        for t in range(1, 8):
-            total = total + slices[t] * weights[k, t]
-        out_ref[k] = total
+        out_ref[k] = totals[k]
 
 
 def shards(occupied, virtual_green, occ_mask, virt_mask, chi_mask, cosine_weights):

time: 53.7 us -> 53.5 us (level)
  no operation moved by 1% of the time
where the time goes in v5:
time: 53.5 us; the launch traced here: 53.3 us
  Pallas kernels  52.6 us (98%)
  local copies, waits for them, and re-layouts  0.66 us (1%)
    pallas_call x1, Pallas kernels, shards(): pl.pallas_call(kernel, out_shape=pltpu.VMEM((8, 16, 256), jnp.float32), i...  52.6 us

profile of v5, /device:TPU:24, one launch (start us, length us, event | category | flops | bytes accessed | tf_op | source)
XLA Modules:
  0.0 53.3 jit_solution(17087340958893014137)
XLA Ops:
  0.0 52.6 %polarizability.1 = f32[8,16,256]{2,1,0:T(8,128)S(1)} custom-call(bf16[1,128,1024]{2,1,0:T(8,128)(2,1)} %occ_hbm.1, bf16[1,1024,256]{2,1,0:T(8,128)(2,1)} %virt_hbm.1, s32[1,8]{1,0:T(1,128)} %occ_mask_hbm.1, s32[2,8]{1,0:T(2,128)} %bitcast.1, s32[1,2]{1,0:T(1,128)} %chi_mask_hbm.1, f32[8,8]{1,0:T(8,128)} %weights_hbm.1), custom_call_target="tpu_custom_call" | custom-call | tf_op jit(solution)/shard_map/polarizability/pallas_call | solution.py:290
  52.7 0.7 %copy.8 = f32[8,16,256]{2,1,0:T(8,128)} copy(f32[8,16,256]{2,1,0:T(8,128)S(1)} %polarizability.1) | data formatting | bytes 262144

commit v6 on v5

--- a/solution.py
+++ b/solution.py
@@ -9,7 +9,8 @@
 
 MESH = pl.DeviceIdType.MESH
 CH = 8
-AHEAD = 3
+LEAD = (3, 3, 2, 3, 3, 2, 3, 3)
+AHEAD = max(LEAD)
 OFFS = (2, 1, 3)
 
 
@@ -120,8 +121,19 @@
             device_id=(to, row, col), device_id_type=MESH,
         )
 
-    for c in range(AHEAD):
-        z_copy(c).start()
+    ahead = sum(jnp.where(tau == t, LEAD[t], 0) for t in range(8))
+
+    def z_start(step):
+        for count in sorted(set(LEAD)):
+            first = 0 if step < 0 else count + step
+            last = count if step < 0 else CH if step == 5 else count + step + 1
+            if first < CH:
+                @pl.when(ahead == count)
+                def _():
+                    for c in range(first, min(last, CH)):
+                        z_copy(c).start()
+
+    z_start(-1)
     for c in range(AHEAD, CH):
         masked(c)
     for i in range(3):
@@ -195,8 +207,7 @@
             if k < 2:
                 y_copy(way, k + 4).start()
             d_copy(way, k).start()
-        if k + AHEAD < CH:
-            z_copy(k + AHEAD).start()
+        z_start(k)
 
     def d_arrived(k):
         for way in range(2):

time: 53.5 us -> 53.1 us (level)
  Pallas kernels: 52.6 us -> 51.7 us
    pallas_call x1, Pallas kernels: 52.6 us -> 51.7 us  [shards(): pl.pallas_call(kernel, out_shape=pltpu.VMEM((8, 16, 256), jnp.float32), i...]
where the time goes in v6:
time: 53.1 us; the launch traced here: 52.4 us
  Pallas kernels  51.7 us (97%)
  local copies, waits for them, and re-layouts  0.66 us (1%)
    pallas_call x1, Pallas kernels, shards(): pl.pallas_call(kernel, out_shape=pltpu.VMEM((8, 16, 256), jnp.float32), i...  51.7 us

profile of v6, /device:TPU:24, one launch (start us, length us, event | category | flops | bytes accessed | tf_op | source)
XLA Modules:
  0.0 52.4 jit_solution(14185806792333293427)
XLA Ops:
  0.0 51.7 %polarizability.1 = f32[8,16,256]{2,1,0:T(8,128)S(1)} custom-call(bf16[1,128,1024]{2,1,0:T(8,128)(2,1)} %occ_hbm.1, bf16[1,1024,256]{2,1,0:T(8,128)(2,1)} %virt_hbm.1, s32[1,8]{1,0:T(1,128)} %occ_mask_hbm.1, s32[2,8]{1,0:T(2,128)} %bitcast.1, s32[1,2]{1,0:T(1,128)} %chi_mask_hbm.1, f32[8,8]{1,0:T(8,128)} %weights_hbm.1), custom_call_target="tpu_custom_call" | custom-call | tf_op jit(solution)/shard_map/polarizability/pallas_call | solution.py:301
  51.7 0.7 %copy.8 = f32[8,16,256]{2,1,0:T(8,128)} copy(f32[8,16,256]{2,1,0:T(8,128)S(1)} %polarizability.1) | data formatting | bytes 262144

commit v7 on v6

--- a/solution.py
+++ b/solution.py
@@ -9,7 +9,7 @@
 
 MESH = pl.DeviceIdType.MESH
 CH = 8
-LEAD = (3, 3, 2, 3, 3, 2, 3, 3)
+LEAD = (3, 3, 2, 2, 2, 2, 3, 3)
 AHEAD = max(LEAD)
 OFFS = (2, 1, 3)
 

time: 53.1 us -> 52.8 us (level)
  no operation moved by 1% of the time
where the time goes in v7:
time: 52.8 us; the launch traced here: 51.9 us
  Pallas kernels  51.2 us (97%)
  local copies, waits for them, and re-layouts  0.66 us (1%)
    pallas_call x1, Pallas kernels, shards(): pl.pallas_call(kernel, out_shape=pltpu.VMEM((8, 16, 256), jnp.float32), i...  51.2 us

profile of v7, /device:TPU:24, one launch (start us, length us, event | category | flops | bytes accessed | tf_op | source)
XLA Modules:
  0.0 51.9 jit_solution(7609036405803367474)
XLA Ops:
  0.0 51.2 %polarizability.1 = f32[8,16,256]{2,1,0:T(8,128)S(1)} custom-call(bf16[1,128,1024]{2,1,0:T(8,128)(2,1)} %occ_hbm.1, bf16[1,1024,256]{2,1,0:T(8,128)(2,1)} %virt_hbm.1, s32[1,8]{1,0:T(1,128)} %occ_mask_hbm.1, s32[2,8]{1,0:T(2,128)} %bitcast.1, s32[1,2]{1,0:T(1,128)} %chi_mask_hbm.1, f32[8,8]{1,0:T(8,128)} %weights_hbm.1), custom_call_target="tpu_custom_call" | custom-call | tf_op jit(solution)/shard_map/polarizability/pallas_call | solution.py:301
  51.2 0.7 %copy.8 = f32[8,16,256]{2,1,0:T(8,128)} copy(f32[8,16,256]{2,1,0:T(8,128)S(1)} %polarizability.1) | data formatting | bytes 262144
